TPU v7x, 32 devices: a whole 2x2x4 slice. The times are simulated.
32 devices in a mesh: vocab: 8 (over z, y), batch: 4 (over x, core).
Axes of the slice: x: 2, y: 2, z: 4, core: 2. Of those that a mesh axis runs over, the one named last changes fastest.
Arguments:
- latent_state_rows: bfloat16 [64, 8192], P('batch', 'vocab'), may hold values from -90 to 90
- closing_rescale_coeffs: bfloat16 [8192], replicated, may hold values from 0.5 to 1.5
- output_projection_matrix: bfloat16 [8192, 131072], P(None, ('vocab', 'batch')), may hold values from -3.7565048 to 3.7565048
- config_heat_values: float32 [16], replicated, may hold values from 0.7 to 1.4
- sequence_config_choice: int32 [64], replicated, may hold values from 0 to 15
- ranked_choice_ids: int32 [64, 128], replicated, may hold values from 0 to 131071
- keep_count: int32 [64], replicated, may hold values from 2 to 128
Outputs:
- log_norm: float32 [64], P('batch')
- kept_mass: float32 [64], P('batch')
- renormed: float32 [64, 128], P('batch')
All inputs are finite; a program needn't handle non-finite values.
Results may differ from a plain program's by a relative error of at most 0.0048.
Values may be sent and summed in bfloat16 or wider, within the bound.
A program may use at most 128 MiB of HBM per device.

v0:
```python
import jax
import jax.numpy as jnp
from jax import lax
from jax.sharding import PartitionSpec as P

epsilon = 1e-06


def normalize(values, gain_part, mean_square):
    factor = lax.rsqrt(mean_square + epsilon)
    return (values * factor[:, None] * gain_part[None, :]).astype(jnp.bfloat16)


def rows_normed(raw_rows, gain_full):
    values = raw_rows.astype(jnp.float32)
    return normalize(values, gain_full, jnp.mean(values * values, axis=1))


def local(
    latent_state_rows,
    closing_rescale_coeffs,
    output_projection_matrix,
    config_heat_values,
    sequence_config_choice,
    ranked_choice_ids,
    keep_count,
):
    group_rows = latent_state_rows.shape[0]
    col_count = output_projection_matrix.shape[1]
    batch_count = lax.axis_size("batch")
    vocab_pos = lax.axis_index("vocab")
    batch_pos = lax.axis_index("batch")
    gain_full = closing_rescale_coeffs.astype(jnp.float32)
    wide_rows = lax.all_gather(latent_state_rows, "vocab", axis=1, tiled=True)
    unnormalized_scores = jnp.dot(
        rows_normed(lax.all_gather(wide_rows, "batch", axis=0, tiled=True), gain_full),
        output_projection_matrix,
        preferred_element_type=jnp.float32,
    )
    config_membership = (
        sequence_config_choice[:, None]
        == jnp.arange(config_heat_values.shape[0], dtype=jnp.int32)[None, :]
    ).astype(jnp.float32)
    sequence_heat_values = jnp.sum(config_membership * config_heat_values[None, :], axis=1)
    divided_scores = unnormalized_scores / sequence_heat_values[:, None]
    offset = (vocab_pos * batch_count + batch_pos) * col_count
    local_ids = ranked_choice_ids - offset
    owned = (local_ids >= 0) & (local_ids < col_count)
    picked = jnp.take_along_axis(divided_scores, jnp.clip(local_ids, 0, col_count - 1), axis=1)
    cand_local = jnp.where(owned, picked, jnp.float32(0.0))
    local_top = jnp.max(divided_scores, axis=1)
    first_slot = batch_pos * group_rows
    row_top = lax.pmax(local_top, ("vocab", "batch"))
    row_total = lax.psum(
        jnp.sum(jnp.exp(divided_scores - row_top[:, None]), axis=1), ("vocab", "batch")
    )
    cand_logit = lax.psum(cand_local, ("vocab", "batch"))
    own_top = lax.dynamic_slice_in_dim(row_top, first_slot, group_rows)
    own_total = lax.dynamic_slice_in_dim(row_total, first_slot, group_rows)
    own_cand = lax.dynamic_slice_in_dim(cand_logit, first_slot, group_rows, 0)
    own_cutoff = lax.dynamic_slice_in_dim(keep_count, first_slot, group_rows)
    log_norm = own_top + jnp.log(own_total)
    kept_mask = jnp.arange(own_cand.shape[1], dtype=jnp.int32)[None, :] < own_cutoff[:, None]
    kept_top = jnp.max(jnp.where(kept_mask, own_cand, jnp.float32(-3e38)), axis=1)
    shifted = jnp.where(kept_mask, own_cand - kept_top[:, None], jnp.float32(0.0))
    kept_exp = jnp.where(kept_mask, jnp.exp(shifted), jnp.float32(0.0))
    kept_sum = jnp.sum(kept_exp, axis=1)
    kept_mass = kept_top + jnp.log(kept_sum) - log_norm
    return (log_norm, kept_mass, kept_exp / kept_sum[:, None])


def solution(mesh):
    placed = (P("batch", "vocab"), P(), P(None, ("vocab", "batch")), P(), P(), P(), P())
    return jax.shard_map(
        local,
        mesh=mesh,
        in_specs=placed,
        out_specs=(P("batch"), P("batch"), P("batch", None)),
        check_vma=False,
    )
```

profile of v0, /device:TPU:0, one launch (start us, length us, event | category | flops | bytes accessed | tf_op | source)
XLA Modules:
  0.0 239.7 jit_solution(4070689631893379016)
XLA Ops:
  7.2 0.0 all-gather.2.cloned.1.call-start
  7.2 34.8 %all_gather.6 = bf16[16,8192]{1,0:T(8,128)(2,1)} all-gather(bf16[16,1024]{1,0:T(8,128)(2,1)} %param.7), channel_id=1, replica_groups=mesh['vocab'=8,'batch'=4] {'vocab'}, dimensions={1}, use_global_device_ids=true | all-gather | bytes 294912 | tf_op jit(solution)/shard_map/all_gather | solution.py:34
  42.0 0.0 all-gather.2.cloned.1.call-update
  42.0 0.7 convert_element_type.11
  42.7 0.7 dynamic_slice.14
  43.5 0.8 select_reduce_fusion.1
  44.2 0.8 fusion.7
  45.0 14.8 %all-gather.2.cloned.1.call-done = bf16[64,8192]{1,0:T(8,128)(2,1)} async-done(((bf16[16,8192]{1,0:T(8,128)(2,1)}), bf16[64,8192]{1,0:T(8,128)(2,1)}) %all-gather.2.cloned.1.call-update) | async-done | bytes 1048592 | tf_op jit(solution)/shard_map/all_gather | solution.py:36
  59.8 1.5 fusion
  61.3 23.9 %fusion.10 = (f32[64]{0:T(128)S(1)}, f32[64,4096]{1,0:T(8,128)S(1)}) fusion(f32[64]{0:T(128)S(1)} %select_reduce_fusion.1, bf16[8192,4096]{1,0:T(8,128)(2,1)} %param.9, bf16[64,8192]{1,0:T(8,128)(2,1)} %all-gather.2.cloned.1.call-done, f32[8192]{0:T(1024)S(1)} %convert_element_type.11, f32[64]{0:T(128)S(1)} %add_rsqrt_fusion), kind=kOutput, calls=%fused_computation.25 | convolution fusion | flops 4297588736 | bytes 69239552 | tf_op jit(solution)/shard_map/dot_general | solution.py:35
  85.2 0.0 copy-start
  85.2 65.0 %gather_fusion = f32[8192]{0:T(1024)S(1)} fusion(f32[64,4096]{1,0:T(8,128)S(1)} %get-tuple-element.8, s32[8192]{0:T(1024)S(1)} %fusion.7), kind=kCustom, calls=%fused_computation | custom fusion | bytes 131072 | tf_op jit(solution)/shard_map/jit(take_along_axis)/gather | solution.py:49
  150.3 0.0 copy-done
  150.3 39.3 %pmax.7 = f32[64]{0:T(128)S(1)} all-reduce(f32[64]{0:T(128)S(1)} %get-tuple-element.7), channel_id=1, replica_groups=mesh['vocab'=8,'batch'=4] {'vocab','batch'}, use_global_device_ids=true, to_apply=%region_3.4 | all-reduce | flops 64 | bytes 512 | tf_op jit(solution)/shard_map/pmax | solution.py:53
  189.6 0.3 exponential_reduce_fusion
  189.9 41.3 %all-reduce = (f32[64]{0:T(128)S(1)}, f32[64,128]{1,0:T(8,128)S(1)}) all-reduce(f32[64]{0:T(128)S(1)} %exponential_reduce_fusion, f32[64,128]{1,0:T(8,128)S(1)} %fusion.6), channel_id=1, replica_groups=mesh['vocab'=8,'batch'=4] {'vocab','batch'}, use_global_device_ids=true, to_apply=%region_5.6 | all-reduce | flops 8256 | bytes 66048 | tf_op jit(solution)/shard_map/psum | solution.py:54
  231.2 0.2 select_reduce_fusion
  231.4 0.2 fusion.9
  231.6 0.7 fusion.8
  232.3 0.6 add_subtract_fusion
  (2 shorter events, 0.0 us)
Async XLA Ops:
  7.2 52.6 %all-gather.2.cloned.1.call-start = ((), (), s32[]{:S(2)}) async-start(), calls=%async_computation | async-start | bytes 1310720 | tf_op jit(solution)/shard_map/all_gather | solution.py:36
  85.2 65.0 %copy-start = (s32[64,128]{1,0:T(8,128)S(1)}, s32[64,128]{1,0:T(8,128)}, u32[]{:S(2)}) copy-start(s32[64,128]{1,0:T(8,128)} %param.12) | copy-start | bytes 98308
Sparse Core Ops, SparseCore 0:
  42.1 17.5 all-gather.1
where the time goes:
time: 240 us
  blocking collectives  115 us (48%)
  local copies, waits for them, and re-layouts  65.7 us (27%)
  matrix products  23.9 us (10%)
  waiting for transfers between devices  14.8 us (6%)
  between operations  14.1 us (6%)
  other arithmetic  5.8 us (2%)
    gather x1, local copies, waits for them, and re-layouts, local(): jnp.take_along_axis(divided_scores, jnp.clip(local_ids, 0, col_count - 1)...  65 us
    psum x1, blocking collectives, local(): lax.psum(jnp.sum(jnp.exp(divided_scores - row_top[:, None]), axis=1), ('v...  41.3 us
    pmax x1, blocking collectives, local(): row_top = lax.pmax(local_top, ('vocab', 'batch'))  39.3 us
    all_gather x1, blocking collectives, local(): wide_rows = lax.all_gather(latent_state_rows, 'vocab', axis=1, tiled=True)  34.8 us
    dot_general x1, matrix products, local(): jnp.dot(rows_normed(lax.all_gather(wide_rows, 'batch', axis=0, tiled=True...  23.9 us
    all_gather x1, waiting for transfers between devices, local(): lax.all_gather(wide_rows, 'batch', axis=0, tiled=True)  14.8 us
  transfers between devices with their start and end apart: 1, of which 1 were waited for; matrix products, arithmetic and copies ran while one was open for 1% of the time, Pallas kernels for 0%

commit v1 on v0

v1 whole, which is shorter than its diff:
```python
import functools

import jax
import jax.numpy as jnp
from jax import lax
from jax.experimental import pallas as pl
from jax.experimental.pallas import tpu as pltpu
from jax.sharding import PartitionSpec as P

MESH = pl.DeviceIdType.MESH
epsilon = 1e-06
LANES = 128
STAT_ROWS = 8
CHUNK_ROWS = 512
STREAM_BYTES = 48 * 1024 * 1024


def iota(shape, axis):
    return lax.broadcasted_iota(jnp.int32, shape, axis)


def column_to_row(column):
    rows = column.shape[0]
    diagonal = iota((rows, LANES), 0) == iota((rows, LANES), 1)
    return jnp.sum(jnp.where(diagonal, column, 0.0), axis=0, keepdims=True)


def row_to_column(row, first, rows):
    width = row.shape[1]
    diagonal = iota((rows, width), 0) + first == iota((rows, width), 1)
    return jnp.sum(jnp.where(diagonal, row, 0.0), axis=1, keepdims=True)


def combine(parts, group):
    candidates = parts[0][:group, :]
    top = parts[0][group : group + 1, :]
    for part in parts[1:]:
        candidates = candidates + part[:group, :]
        top = jnp.maximum(top, part[group : group + 1, :])
    total = jnp.zeros_like(top)
    for part in parts:
        total = total + part[group + 1 : group + 2, :] * jnp.exp(
            part[group : group + 1, :] - top
        )
    return candidates, top, total


def kernel(
    n_v,
    n_b,
    n_slots,
    kc,
    x_ref,
    gain_ref,
    w_ref,
    heat_ref,
    choice_ref,
    ids_ref,
    keep_ref,
    norm_ref,
    mass_ref,
    renorm_ref,
    wbuf,
    xbuf,
    lhs,
    acc,
    outbox,
    inbox,
    midbox,
    lastbox,
    w_sem,
    x_recv,
    a_send,
    x_send,
    c_send,
    t_send,
    t_recv,
    u_send,
    u_recv,
):
    v = lax.axis_index("vocab")
    b = lax.axis_index("batch")
    n_x = n_b // 2
    x = b // 2
    c = b % 2
    partner = 2 * x + (1 - c)
    group, fpd = x_ref.shape
    slots = n_b * group
    depth, cols = w_ref.shape
    n_k = depth // kc
    per_block = fpd // kc

    def stream(k):
        slot = lax.rem(k, n_slots)
        return pltpu.make_async_copy(
            w_ref.at[pl.ds(pl.multiple_of(k * kc, kc), kc), :], wbuf.at[slot], w_sem.at[slot]
        )

    for k in range(n_slots):
        stream(k).start()

    barrier = pltpu.get_barrier_semaphore()
    for j in range(1, n_v):
        pl.semaphore_signal(barrier, inc=1, device_id=((v + j) % n_v, b), device_id_type=MESH)
    for j in range(1, n_b):
        pl.semaphore_signal(barrier, inc=1, device_id=(v, (b + j) % n_b), device_id_type=MESH)
    pl.semaphore_wait(barrier, n_v - 1 + n_b - 1)

    def send(src, dst, send_sem, recv_sem, to):
        copy = pltpu.make_async_remote_copy(
            src_ref=src,
            dst_ref=dst,
            send_sem=send_sem,
            recv_sem=recv_sem,
            device_id=to,
            device_id_type=MESH,
        )
        copy.start()
        return copy

    def arrived(row, col):
        pltpu.make_async_copy(x_ref, xbuf.at[row, col], x_recv.at[row, col]).wait()

    sent = []
    for j in range(1, n_v):
        sent.append(
            send(x_ref, xbuf.at[b, v], a_send.at[j], x_recv.at[b, v], ((v + j) % n_v, b))
        )
    for j in range(n_v):
        origin = (v - j + n_v) % n_v
        block = x_ref if j == 0 else xbuf.at[b, origin]
        if j > 0:
            arrived(b, origin)
        for i in range(1, n_x):
            to = 2 * ((x + i) % n_x) + c
            sent.append(
                send(block, xbuf.at[b, origin], x_send.at[i, j], x_recv.at[b, origin], (v, to))
            )
        sent.append(
            send(block, xbuf.at[b, origin], c_send.at[0, j], x_recv.at[b, origin], (v, partner))
        )
    for j in range(n_v):
        for i in range(1, n_x):
            origin = (v - j + n_v) % n_v
            source = 2 * ((x - i + n_x) % n_x) + c
            arrived(source, origin)
            block = xbuf.at[source, origin]
            sent.append(
                send(block, block, c_send.at[i, j], x_recv.at[source, origin], (v, partner))
            )
    for j in range(n_v):
        for i in range(n_x):
            origin = (v - j + n_v) % n_v
            source = 2 * ((x - i + n_x) % n_x) + (1 - c)
            arrived(source, origin)
    xbuf[b, v] = x_ref[...]

    def square(f, carry):
        values = xbuf[:, f].reshape(slots, fpd).astype(jnp.float32)
        values = values * values
        for t in range(fpd // LANES):
            carry = carry + values[:, t * LANES : (t + 1) * LANES]
        return carry

    squares = lax.fori_loop(0, n_v, square, jnp.zeros((slots, LANES), jnp.float32))
    mean_square = jnp.sum(squares, axis=1, keepdims=True) / depth
    factor = lax.rsqrt(mean_square + epsilon)

    def rescale(f, carry):
        values = xbuf[:, f].reshape(slots, fpd).astype(jnp.float32)
        gain = gain_ref[pl.ds(f, 1), :]
        normed = (values * factor * gain).astype(jnp.bfloat16)
        for i in range(per_block):
            lhs[f * per_block + i] = normed[:, i * kc : (i + 1) * kc]
        return carry

    lax.fori_loop(0, n_v, rescale, 0)

    acc[...] = jnp.zeros_like(acc)

    def multiply(k, carry):
        slot = lax.rem(k, n_slots)
        stream(k).wait()
        acc[...] += jnp.dot(lhs[k], wbuf[slot], preferred_element_type=jnp.float32)

        @pl.when(k + n_slots < n_k)
        def _():
            stream(k + n_slots).start()

        return carry

    lax.fori_loop(0, n_k, multiply, 0)

    choice = row_to_column(choice_ref[...].astype(jnp.float32), 0, slots)
    n_heat = heat_ref.shape[1]
    member = choice == iota((slots, n_heat), 1).astype(jnp.float32)
    heat = jnp.sum(jnp.where(member, heat_ref[...], 0.0), axis=1, keepdims=True)

    local_ids = ids_ref[...] - (v * n_b + b) * cols
    tile_of = local_ids >> 7
    lane_of = local_ids & (LANES - 1)
    picked = jnp.zeros((slots, LANES), jnp.float32)
    top = jnp.full((slots, LANES), -3e38, jnp.float32)
    for t in range(cols // LANES):
        part = acc[:, t * LANES : (t + 1) * LANES] / heat
        acc[:, t * LANES : (t + 1) * LANES] = part
        top = jnp.maximum(top, part)
        found = jnp.take_along_axis(part, lane_of, axis=1, mode="promise_in_bounds")
        picked = jnp.where(tile_of == t, found, picked)
    top = jnp.max(top, axis=1, keepdims=True)
    total = jnp.zeros((slots, LANES), jnp.float32)
    for t in range(cols // LANES):
        total = total + jnp.exp(acc[:, t * LANES : (t + 1) * LANES] - top)
    total = jnp.sum(total, axis=1, keepdims=True)

    for p in range(n_b):
        rows = slice(p * group, (p + 1) * group)
        outbox[p, :group, :] = picked[rows, :]
        outbox[p, group : group + 1, :] = column_to_row(top[rows, :])
        outbox[p, group + 1 : group + 2, :] = column_to_row(total[rows, :])
        outbox[p, group + 2 :, :] = jnp.zeros((STAT_ROWS - 2, LANES), jnp.float32)
    for j in range(1, n_b):
        to = (b + j) % n_b
        sent.append(send(outbox.at[to], inbox.at[b], t_send.at[j], t_recv.at[b], (v, to)))
    parts = [outbox[b]]
    for j in range(1, n_b):
        source = (b - j + n_b) % n_b
        pltpu.make_async_copy(outbox.at[0], inbox.at[source], t_recv.at[source]).wait()
        parts.append(inbox[source])
    candidates, top, total = combine(parts, group)
    midbox[:group, :] = candidates
    midbox[group : group + 1, :] = top
    midbox[group + 1 : group + 2, :] = total
    midbox[group + 2 :, :] = jnp.zeros((STAT_ROWS - 2, LANES), jnp.float32)
    for j in range(1, n_v):
        to = (v + j) % n_v
        sent.append(send(midbox, lastbox.at[v], u_send.at[j], u_recv.at[v], (to, b)))
    lastbox[v] = midbox[...]
    for j in range(1, n_v):
        source = (v - j + n_v) % n_v
        pltpu.make_async_copy(midbox, lastbox.at[source], u_recv.at[source]).wait()
    candidates, top, total = combine([lastbox[s] for s in range(n_v)], group)

    log_norm = top + jnp.log(jnp.where(total > 0.0, total, 1.0))
    cutoff = row_to_column(keep_ref[...].astype(jnp.float32), b * group, group)
    kept = iota((group, LANES), 1).astype(jnp.float32) < cutoff
    kept_top = jnp.max(jnp.where(kept, candidates, -3e38), axis=1, keepdims=True)
    shifted = jnp.where(kept, candidates - kept_top, 0.0)
    kept_exp = jnp.where(kept, jnp.exp(shifted), 0.0)
    kept_sum = jnp.sum(kept_exp, axis=1, keepdims=True)
    kept_log = column_to_row(kept_top + jnp.log(kept_sum))
    norm_ref[...] = log_norm[:, :group]
    mass_ref[...] = (kept_log - log_norm)[:, :group]
    renorm_ref[...] = kept_exp / kept_sum
    for copy in sent:
        copy.wait_send()


def solution(mesh):
    n_v, n_b = mesh.shape["vocab"], mesh.shape["batch"]

    def local(rows, gain, w, heat, choice, ids, keep):
        group, fpd = rows.shape
        depth, cols = w.shape
        slots = n_b * group
        kc = min(fpd, CHUNK_ROWS)
        n_slots = min(depth // kc, max(1, STREAM_BYTES // (kc * cols * 2)))
        box = group + STAT_ROWS
        vmem = pl.BlockSpec(memory_space=pltpu.VMEM)
        log_norm, mass, renormed = pl.pallas_call(
            functools.partial(kernel, n_v, n_b, n_slots, kc),
            out_shape=(
                jax.ShapeDtypeStruct((1, group), jnp.float32),
                jax.ShapeDtypeStruct((1, group), jnp.float32),
                jax.ShapeDtypeStruct((group, ids.shape[1]), jnp.float32),
            ),
            in_specs=[vmem, vmem, pl.BlockSpec(memory_space=pl.ANY), vmem, vmem, vmem, vmem],
            out_specs=(vmem, vmem, vmem),
            scratch_shapes=[
                pltpu.VMEM((n_slots, kc, cols), jnp.bfloat16),
                pltpu.VMEM((n_b, n_v, group, fpd), jnp.bfloat16),
                pltpu.VMEM((depth // kc, slots, kc), jnp.bfloat16),
                pltpu.VMEM((slots, cols), jnp.float32),
                pltpu.VMEM((n_b, box, LANES), jnp.float32),
                pltpu.VMEM((n_b, box, LANES), jnp.float32),
                pltpu.VMEM((box, LANES), jnp.float32),
                pltpu.VMEM((n_v, box, LANES), jnp.float32),
                pltpu.SemaphoreType.DMA((n_slots,)),
                pltpu.SemaphoreType.DMA((n_b, n_v)),
                pltpu.SemaphoreType.DMA((n_v,)),
                pltpu.SemaphoreType.DMA((n_b // 2, n_v)),
                pltpu.SemaphoreType.DMA((n_b // 2, n_v)),
                pltpu.SemaphoreType.DMA((n_b,)),
                pltpu.SemaphoreType.DMA((n_b,)),
                pltpu.SemaphoreType.DMA((n_v,)),
                pltpu.SemaphoreType.DMA((n_v,)),
            ],
            compiler_params=pltpu.CompilerParams(
                collective_id=0,
                has_side_effects=True,
                vmem_limit_bytes=60 * 1024 * 1024,
            ),
        )(
            rows,
            gain.astype(jnp.float32).reshape(n_v, fpd),
            w,
            heat.reshape(1, -1),
            choice.reshape(1, -1),
            ids,
            keep.reshape(1, -1),
        )
        return log_norm.reshape(group), mass.reshape(group), renormed

    placed = (P("batch", "vocab"), P(), P(None, ("vocab", "batch")), P(), P(), P(), P())
    return jax.shard_map(
        local,
        mesh=mesh,
        in_specs=placed,
        out_specs=(P("batch"), P("batch"), P("batch", None)),
        check_vma=False,
    )
```

time: 240 us -> 48.4 us (0.20)
  blocking collectives: 115 us -> 0 us
  local copies, waits for them, and re-layouts: 65.7 us -> 4.91 us
  Pallas kernels: 0 us -> 42.5 us
  matrix products: 23.9 us -> 0 us
  waiting for transfers between devices: 14.8 us -> 0 us
  between operations: 14.1 us -> 0.64 us
  other arithmetic: 5.8 us -> 0 us
    gather x1 -> x0, local copies, waits for them, and re-layouts: 65 us -> none  [local(): jnp.take_along_axis(divided_scores, jnp.clip(local_ids, 0, col_count - 1)...]
    pallas_call x0 -> x1, Pallas kernels: none -> 42.5 us  [local(): pl.pallas_call(functools.partial(kernel, n_v, n_b, n_slots, kc), out_shap...]
    psum x1 -> x0, blocking collectives: 41.3 us -> none  [local(): lax.psum(jnp.sum(jnp.exp(divided_scores - row_top[:, None]), axis=1), ('v...]
    pmax x1 -> x0, blocking collectives: 39.3 us -> none  [local(): row_top = lax.pmax(local_top, ('vocab', 'batch'))]
    all_gather x1 -> x0, blocking collectives: 34.8 us -> none  [local(): wide_rows = lax.all_gather(latent_state_rows, 'vocab', axis=1, tiled=True)]
    dot_general x1 -> x0, matrix products: 23.9 us -> none  [local(): jnp.dot(rows_normed(lax.all_gather(wide_rows, 'batch', axis=0, tiled=True...]
    all_gather x1 -> x0, waiting for transfers between devices: 14.8 us -> none  [local(): lax.all_gather(wide_rows, 'batch', axis=0, tiled=True)]
    unnamed x2 -> x3, local copies, waits for them, and re-layouts: 0.01 us -> 3.56 us
  transfers between devices with their start and end apart: 1 -> 0, of which waited for: 1 -> 0; matrix products, arithmetic and copies ran while one was open for 1% -> 0% of each run, Pallas kernels for 0% -> 0%
where the time goes in v1:
time: 48.4 us; the launch traced here: 48.1 us
  Pallas kernels  42.5 us (88%)
  local copies, waits for them, and re-layouts  4.91 us (10%)
  between operations  0.64 us (1%)
    pallas_call x1, Pallas kernels, local(): pl.pallas_call(functools.partial(kernel, n_v, n_b, n_slots, kc), out_shap...  42.5 us
    unnamed x3, local copies, waits for them, and re-layouts  3.56 us
    reshape x1, local copies, waits for them, and re-layouts, local(): gain.astype(jnp.float32).reshape(n_v, fpd)  1.35 us

profile of v1, /device:TPU:0, one launch (start us, length us, event | category | flops | bytes accessed | tf_op | source)
XLA Modules:
  0.0 48.1 jit_solution(5117862312247617412)
XLA Ops:
  0.6 1.3 %reshape.34.gain_ref = f32[8,1024]{1,0:T(8,128)} reshape(bf16[8192]{0:T(1024)(128)(2,1)} %param.8) | data formatting | bytes 49152 | tf_op jit(solution)/shard_map/reshape | solution.py:305
  2.0 42.5 %shard_map.94 = (f32[1,16]{1,0:T(1,128)}, f32[1,16]{1,0:T(1,128)}, f32[16,128]{1,0:T(8,128)}) custom-call(bf16[16,1024]{1,0:T(8,128)(2,1)} %x_ref.1, f32[8,1024]{1,0:T(8,128)} %reshape.34.gain_ref, bf16[8192,4096]{1,0:T(8,128)(2,1)} %w_ref.1, f32[1,16]{1,0:T(1,128)} %bitcast.5, s32[1,64]{1,0:T(1,128)} %bitcast.6, s32[64,128]{1,0:T(8,128)} %ids_ref.1, ...), custom_call_target="tpu_custom_call" | custom-call | tf_op jit(solution)/shard_map/pallas_call | solution.py:270
  44.5 1.1 %copy.13 = f32[16]{0:T(128)} copy(f32[16]{0:T(128)} %bitcast.9) | data formatting | bytes 128
  45.6 1.1 %copy.14 = f32[16]{0:T(128)} copy(f32[16]{0:T(128)} %bitcast.8) | data formatting | bytes 128
  46.8 1.3 %copy.15 = f32[16,128]{1,0:T(8,128)} copy(f32[16,128]{1,0:T(8,128)} %get-tuple-element.14) | data formatting | bytes 16384
